TPU v7x, 512 devices: a whole 4x8x8 slice. The times are simulated.
512 devices in a mesh: row: 32 (over z, x), col: 16 (over y, core).
Axes of the slice: x: 4, y: 8, z: 8, core: 2. Of those that a mesh axis runs over, the one named last changes fastest.
Arguments:
- lower: bfloat16 [32, 3, 512, 2, 512], P('row', None, None, None, 'col'), as said below
- rhs: bfloat16 [32, 3, 512, 8192], P('row', None, None, 'col'), may hold values from -6 to 6
- tile_map: int32 [16], replicated, may hold values from 0 to 15, each once
Outputs:
- overwritten: bfloat16 [32, 3, 512, 8192], P('row', None, None, 'col')
Inputs may be any that keep to these rules, and one draw needn't show every extreme that they name: tile_map is a permutation of 0 to 15. lower[0, 0, :, 0, :] and lower[1, 0, :, 1, :] are lower triangular with diagonal entries between 2 and 3; lower[0, 0, :, 1, :] is zero.
All inputs are finite; a program needn't handle non-finite values.
Results may differ from a plain program's by a relative error of at most 0.0032.
Values may be sent and summed in bfloat16 or wider, within the bound.
A program may use at most 64 MiB of HBM per device.

v0:
```python
import jax
import jax.numpy as jnp
from jax import lax
from jax.sharding import Mesh
from jax.sharding import PartitionSpec as P

ROW = ("row_0", "row_1")


def spread(shard, axes, root):
    shard = jnp.where(lax.axis_index(axes) == root, shard, jnp.zeros_like(shard))
    for axis in axes:
        shard = lax.psum(shard, axis)
    return shard


def reorder(block, tile_map, tile):
    shape = block.shape
    tiles = block.reshape(shape[:-1] + (shape[-1] // tile, tile))
    return jnp.take(tiles, tile_map, axis=3).reshape(shape)


def body(lower, rhs, tile_map):
    tile = lower.shape[2]
    here = lax.axis_index(ROW)
    whole = lax.all_gather(lower, "col", axis=4, tiled=True)
    panels = whole[0]
    rows = panels.shape[0] * tile
    rhs = lax.all_to_all(
        reorder(
            lax.all_to_all(rhs, "col", split_axis=2, concat_axis=3, tiled=True), tile_map, tile
        ),
        "col",
        split_axis=3,
        concat_axis=2,
        tiled=True,
    )
    work = rhs[0].astype(jnp.float32)
    identity = jnp.eye(tile, dtype=jnp.float32)
    solved_rows = []
    for panel in range(2):
        mine = jnp.where(
            here == panel, jnp.tril(panels[0, :, panel, :].astype(jnp.float32)), identity
        )
        local = jax.scipy.linalg.solve_triangular(mine, work[0], lower=True).astype(jnp.bfloat16)
        solved = spread(local, ROW, panel)
        flat = panels[:, :, panel, :].reshape(rows, tile)
        work = work - jnp.dot(flat, solved, preferred_element_type=jnp.float32).reshape(work.shape)
        solved_rows.append(solved)
    first, second = (solved_rows[0], solved_rows[1])
    result = work.astype(jnp.bfloat16)
    leading = jnp.where(here == 0, first, jnp.where(here == 1, second, result[0]))
    result = result.at[0].set(leading)[None]
    return result


def solution(mesh):
    torus = Mesh(mesh.devices.reshape(8, 4, mesh.shape["col"]), ("row_0", "row_1", "col"))
    return jax.shard_map(
        body,
        mesh=torus,
        in_specs=(P(ROW, None, None, None, "col"), P(ROW, None, None, "col"), P()),
        out_specs=P(ROW, None, None, "col"),
        check_vma=False,
    )
```

profile of v0, /device:TPU:1, one launch (start us, length us, event | category | flops | bytes accessed | tf_op | source)
XLA Modules:
  0.0 520.9 jit_solution(17489380718761430764)
XLA Ops:
  6.5 4.1 copy.38
  10.6 10.5 %all-to-all-start = ((bf16[1,3,512,512]{3,1,0,2:T(4,128)(2,1)}), bf16[1,3,512,512]{3,1,0,2:T(4,128)(2,1)S(1)}, u32[]{:S(2)}, u32[]{:S(2)}) async-start(bf16[1,3,512,512]{3,1,0,2:T(4,128)(2,1)} %copy.38), calls=%async_computation | async-start | bytes 4194304 | tf_op jit(solution)/shard_map/all_to_all | solution.py:31
  22.2 58.7 %all-to-all-done = bf16[1,3,512,512]{3,1,0,2:T(4,128)(2,1)S(1)} async-done(((bf16[1,3,512,512]{3,1,0,2:T(4,128)(2,1)}), bf16[1,3,512,512]{3,1,0,2:T(4,128)(2,1)S(1)}, u32[]{:S(2)}, u32[]{:S(2)}) %all-to-all-start) | async-done | bytes 1572896 | tf_op jit(solution)/shard_map/all_to_all | solution.py:31
  86.4 8.3 %copy.41 = bf16[1,3,32,8192]{2,1,0,3:T(4,128)(2,1)} copy(bf16[1,3,32,8192]{3,2,1,0:T(8,128)(2,1)S(1)} %broadcast_select_fusion) | data formatting | bytes 3145728 | tf_op jit(solution)/shard_map/jit(_take)/select_n | solution.py:20
  94.8 13.2 %reshape.163 = bf16[16,2,24576]{2,1,0:T(2,128)(2,1)} reshape(bf16[8192,1,3,32]{3,2,1,0:T(4,128)(2,1)} %bitcast.122) | data formatting | bytes 3145728
  108.0 6.2 %all-to-all-start.1 = ((bf16[16,2,24576]{2,1,0:T(2,128)(2,1)}), bf16[16,2,24576]{2,1,0:T(2,128)(2,1)}, u32[]{:S(2)}, u32[]{:S(2)}) async-start(bf16[16,2,24576]{2,1,0:T(2,128)(2,1)} %reshape.163), calls=%async_computation.1 | async-start | bytes 3145728 | tf_op jit(solution)/shard_map/all_to_all | solution.py:29
  114.5 7.0 %copy.45 = bf16[1,3,512,2,512]{4,2,3,1,0:T(8,128)(2,1)S(1)} copy(bf16[1,3,512,2,512]{2,3,1,0,4:T(2,128)(2,1)} %all-gather.2.cloned.1.call-done) | data formatting | bytes 6291456 | tf_op jit(solution)/shard_map/all_gather | solution.py:26
  123.8 11.5 %while.5 = (s32[]{:T(128)}, f32[512,512]{1,0:T(8,128)}, s32[4,2]{0,1:T(2,128)S(1)}, f32[4,128,128]{2,1,0:T(8,128)S(1)}, s32[]{:T(128)}) while((s32[]{:T(128)}, f32[512,512]{1,0:T(8,128)}, s32[4,2]{0,1:T(2,128)S(1)}, f32[4,128,128]{2,1,0:T(8,128)S(1)}, s32[]{:T(128)}) %tuple.41), condition=%wide.while_cond.1, body=%wide.while_body.1.sunk | while | flops 2 | bytes 131189 | solution.py:45
  124.4 2.3 bitcast_dynamic-update-slice_fusion.4
  127.3 2.3 bitcast_dynamic-update-slice_fusion.4
  130.2 2.3 bitcast_dynamic-update-slice_fusion.4
  135.3 39.3 %custom-call.4 = f32[4,128,128]{1,2,0:T(8,128)S(1)} custom-call(f32[4,128,128]{2,1,0:T(8,128)S(1)} %get-tuple-element.32), custom_call_target="InvertDiagBlocksLowerTriangular" | custom-call | tf_op jit(solution)/shard_map/jit(_solve_triangular)/triangular_solve | solution.py:45
  174.6 12.6 %reshape.164 = bf16[8192,1,3,32]{3,2,1,0:T(4,128)(2,1)} reshape(bf16[16,2,24576]{2,1,0:T(2,128)(2,1)} %all-to-all-done.1) | data formatting | bytes 3145728
  187.2 9.7 %copy.42 = bf16[1,3,32,8192]{3,2,1,0:T(8,128)(2,1)S(1)} copy(bf16[1,3,32,8192]{2,1,0,3:T(4,128)(2,1)} %bitcast.123) | data formatting | bytes 3145728 | tf_op jit(solution)/shard_map/all_to_all | solution.py:29
  206.0 78.6 %all-reduce.5.cloned.1.call-done = bf16[512,512]{1,0:T(8,128)(2,1)} async-done(((bf16[512,512]{1,0:T(8,128)(2,1)}), bf16[512,512]{1,0:T(8,128)(2,1)}) %all-reduce.5.cloned.1.call-update) | async-done | bytes 524304 | tf_op jit(solution)/shard_map/psum | solution.py:13
  285.5 13.6 %while.6 = (s32[]{:T(128)}, f32[512,512]{1,0:T(8,128)}, s32[4,2]{0,1:T(2,128)S(1)}, f32[4,128,128]{2,1,0:T(8,128)}, s32[]{:T(128)}) while((s32[]{:T(128)}, f32[512,512]{1,0:T(8,128)}, s32[4,2]{0,1:T(2,128)S(1)}, f32[4,128,128]{2,1,0:T(8,128)}, s32[]{:T(128)}) %tuple.57), condition=%wide.while_cond.1.clone, body=%wide.while_body.1.clone.sunk | while | flops 2 | bytes 132205 | solution.py:45
  286.1 2.8 bitcast_dynamic-update-slice_fusion.5
  289.6 2.8 bitcast_dynamic-update-slice_fusion.5
  293.0 2.8 bitcast_dynamic-update-slice_fusion.5
  296.4 2.7 bitcast_dynamic-update-slice_fusion.5
  299.1 3.7 copy.43
  302.8 40.1 %custom-call.5 = f32[4,128,128]{1,2,0:T(8,128)S(1)} custom-call(f32[4,128,128]{2,1,0:T(8,128)} %get-tuple-element.33), custom_call_target="InvertDiagBlocksLowerTriangular" | custom-call | tf_op jit(solution)/shard_map/jit(_solve_triangular)/triangular_solve | solution.py:45
  343.0 4.0 fusion.50
  346.9 4.3 convolution_bitcast_fusion.1
  351.2 3.6 copy.47
  354.8 2.6 sub.25
  364.6 77.8 %all-reduce.9.cloned.1.call-done = bf16[512,512]{1,0:T(8,128)(2,1)} async-done(((bf16[512,512]{1,0:T(8,128)(2,1)}), bf16[512,512]{1,0:T(8,128)(2,1)}) %all-reduce.9.cloned.1.call-update) | async-done | bytes 524304 | tf_op jit(solution)/shard_map/psum | solution.py:13
  442.5 56.1 %all-reduce.11.cloned.1.call-done = bf16[512,512]{1,0:T(8,128)(2,1)} async-done(((bf16[512,512]{1,0:T(8,128)(2,1)}), bf16[512,512]{1,0:T(8,128)(2,1)}) %all-reduce.11.cloned.1.call-update) | async-done | bytes 524304 | tf_op jit(solution)/shard_map/psum | solution.py:13
  498.6 4.3 convolution_bitcast_fusion
  502.9 3.6 copy.50
  506.5 5.2 fusion.1
  511.7 2.7 fusion.21
  (80 shorter events, 33.1 us)
Async XLA Ops:
  10.6 10.5 %copy-start.5 = (bf16[1,3,512,2,32]{2,4,3,1,0:T(8,128)(2,1)S(1)}, bf16[1,3,512,2,32]{2,4,3,1,0:T(8,128)(2,1)}, u32[]{:S(2)}) copy-start(bf16[1,3,512,2,32]{2,4,3,1,0:T(8,128)(2,1)} %param.7) | copy-start | bytes 589828
  10.6 11.5 %copy-start.6 = (s32[16]{0:T(128)S(1)}, s32[16]{0:T(128)}, u32[]{:S(2)}) copy-start(s32[16]{0:T(128)} %param.9) | copy-start | bytes 196
  10.6 70.3 %all-to-all-start = ((bf16[1,3,512,512]{3,1,0,2:T(4,128)(2,1)}), bf16[1,3,512,512]{3,1,0,2:T(4,128)(2,1)S(1)}, u32[]{:S(2)}, u32[]{:S(2)}) async-start(bf16[1,3,512,512]{3,1,0,2:T(4,128)(2,1)} %copy.38), calls=%async_computation | async-start | bytes 4194304 | tf_op jit(solution)/shard_map/all_to_all | solution.py:31
  21.1 93.4 %all-gather.2.cloned.1.call-start = ((), (), s32[]{:S(2)}) async-start(), calls=%async_computation.2 | async-start | bytes 3342336 | tf_op jit(solution)/shard_map/all_gather | solution.py:26
  108.0 66.7 %all-to-all-start.1 = ((bf16[16,2,24576]{2,1,0:T(2,128)(2,1)}), bf16[16,2,24576]{2,1,0:T(2,128)(2,1)}, u32[]{:S(2)}, u32[]{:S(2)}) async-start(bf16[16,2,24576]{2,1,0:T(2,128)(2,1)} %reshape.163), calls=%async_computation.1 | async-start | bytes 3145728 | tf_op jit(solution)/shard_map/all_to_all | solution.py:29
  114.2 170.3 %all-reduce.5.cloned.1.call-start = ((), (), s32[]{:S(2)}) async-start(), calls=%async_computation.3 | async-start | bytes 1048576 | tf_op jit(solution)/shard_map/psum | solution.py:13
  121.5 2.2 copy-start
  197.5 1.7 copy-start.1
  205.9 141.0 %all-reduce.7.cloned.1.call-start = ((), (), s32[]{:S(2)}) async-start(), calls=%async_computation.4 | async-start | bytes 1048576 | tf_op jit(solution)/shard_map/psum | solution.py:13
  284.6 157.9 %all-reduce.9.cloned.1.call-start = ((), (), s32[]{:S(2)}) async-start(), calls=%async_computation.5 | async-start | bytes 1048576 | tf_op jit(solution)/shard_map/psum | solution.py:13
  357.4 1.8 copy-start.2
  364.3 134.3 %all-reduce.11.cloned.1.call-start = ((), (), s32[]{:S(2)}) async-start(), calls=%async_computation.6 | async-start | bytes 1048576 | tf_op jit(solution)/shard_map/psum | solution.py:13
  506.5 5.2 copy-start.3
  506.5 5.2 copy-start.4
Sparse Core Ops, SparseCore 0:
  24.0 65.5 all-gather.1
  206.0 78.4 all-reduce.4
  286.9 53.9 all-reduce.6
  364.4 77.9 all-reduce.8
  444.6 53.9 all-reduce.10
where the time goes:
time: 524 us; the launch traced here: 521 us
  waiting for transfers between devices  271 us (52%)
  local copies, waits for them, and re-layouts  104 us (20%)
  other arithmetic  93.7 us (18%)
  matrix products  20.2 us (4%)
  starting transfers between devices  17.6 us (3%)
  between operations  13.5 us (3%)
    psum x4, waiting for transfers between devices, spread(): shard = lax.psum(shard, axis)  213 us
    another operation x4, other arithmetic, body(): jax.scipy.linalg.solve_triangular(mine, work[0], lower=True)  81.2 us
    all_to_all x1, waiting for transfers between devices, body(): lax.all_to_all(rhs, 'col', split_axis=2, concat_axis=3, tiled=True)  58.7 us
    unnamed x21, local copies, waits for them, and re-layouts  32.9 us
    another operation x27, local copies, waits for them, and re-layouts, body(): jax.scipy.linalg.solve_triangular(mine, work[0], lower=True)  25.7 us
    another operation x14, matrix products, body(): jax.scipy.linalg.solve_triangular(mine, work[0], lower=True)  11.6 us
  transfers between devices with their start and end apart: 7, of which 4 were waited for; matrix products, arithmetic and copies ran while one was open for 29% of the time, Pallas kernels for 0%

commit v1 on v0

v1 whole, which is shorter than its diff:
```python
import functools

import jax
import jax.numpy as jnp
from jax import lax
from jax.experimental import pallas as pl
from jax.experimental.pallas import tpu as pltpu
from jax.sharding import PartitionSpec as P

MESH = pl.DeviceIdType.MESH
BLOCK = 128
HIGHEST = lax.Precision.HIGHEST


def dot_t(a, b):
    return lax.dot_general(a, b, (((0,), (0,)), ((), ())), preferred_element_type=jnp.float32)


def dot_f32(a, b):
    return jnp.dot(a, b, preferred_element_type=jnp.float32, precision=HIGHEST)


def kernel(
    rows, cols, tm_ref, rhs_ref, lt_ref, out_ref,
    a0, a1, a2, t0, t1, t2, c_ref, g_ref, s0_ref, s1_ref, acc_ref, lf_ref, inv_ref, x_ref,
    p1_send, p1_recv, p2_send, p2_recv, up_send, up_recv, down_send, down_recv,
    pair_send, pair_recv, sc_send, sc_recv, ga_send, ga_recv,
):
    a_refs, t_refs = (a0, a1, a2), (t0, t1, t2)
    tiles, tile = rhs_ref.shape[0], rhs_ref.shape[1]
    slab, piece = tile // cols, tile // rows
    chips = cols // 2
    far = chips // 2
    blocks = tile // BLOCK
    row, col = lax.axis_index("row"), lax.axis_index("col")
    chip, core = col // 2, col % 2

    barrier = pltpu.get_barrier_semaphore()

    def greet_col(d, _):
        pl.semaphore_signal(
            barrier, inc=1, device_id={"col": lax.rem(col + d, cols)}, device_id_type=MESH
        )
        return 0

    def greet_row(d, _):
        pl.semaphore_signal(
            barrier, inc=1, device_id={"row": lax.rem(row + d, rows)}, device_id_type=MESH
        )
        return 0

    lax.fori_loop(1, cols, greet_col, 0)
    lax.fori_loop(1, rows, greet_row, 0)
    pl.semaphore_wait(barrier, cols + rows - 2)

    def at_chip(offset):
        return lax.rem(chip + offset + 2 * chips, chips) * 2 + core

    def rows_of(index, size):
        return pl.ds(pl.multiple_of(index * size, size), size)

    def remote(src, dst, send, recv, target):
        copy = pltpu.make_async_remote_copy(
            src_ref=src, dst_ref=dst, send_sem=send, recv_sem=recv,
            device_id=target, device_id_type=MESH,
        )
        copy.start()

    def drain(ref, sem):
        pltpu.make_async_copy(ref, ref, sem).wait()

    partner = {"col": chip * 2 + 1 - core}

    def panel(offset, half=None):
        where = rows_of(at_chip(offset), slab)
        if half is None:
            return g_ref.at[:, :, where, :]
        return g_ref.at[:, half, where, :]

    def send_up(step):
        half = 0 if step == far else None
        block = panel(1 - step, half)
        src = lt_ref if step == 1 else block
        if step == 1 and half is not None:
            src = lt_ref.at[:, half]
        remote(src, block, up_send.at[step - 1], up_recv.at[step - 1], {"col": at_chip(1)})

    def send_down(step):
        half = 1 if step == far else None
        block = panel(step - 1, half)
        src = lt_ref if step == 1 else block
        if step == 1 and half is not None:
            src = lt_ref.at[:, half]
        remote(src, block, down_send.at[step - 1], down_recv.at[step - 1], {"col": at_chip(-1)})

    def arrive(step):
        up = panel(-step, 0 if step == far else None)
        down = panel(step, 1 if step == far else None)
        drain(up, up_recv.at[step - 1])
        drain(down, down_recv.at[step - 1])
        if step < far:
            send_up(step + 1)
            send_down(step + 1)
        remote(up, up, pair_send, pair_recv, partner)
        remote(down, down, pair_send, pair_recv, partner)

    order = []
    for d in range(far, 0, -1):
        order += [d] if d in (far,) else [d, chips - d]
    targets = []
    for d in order:
        targets.append(lax.rem(chip + d, chips) * 2 + core)
        targets.append(lax.rem(chip + d, chips) * 2 + 1 - core)
    targets.append(chip * 2 + 1 - core)

    def phase1(m):
        for p in targets:
            remote(
                rhs_ref.at[m, rows_of(p, slab), :], a_refs[m].at[col],
                p1_send.at[m], p1_recv.at[m], {"col": p},
            )
        a_refs[m][col] = rhs_ref[m, rows_of(col, slab), :]

    def phase2(m):
        drain(a_refs[m].at[pl.ds(0, cols - 1)], p1_recv.at[m])
        for j in range(cols):
            t_refs[m][j] = a_refs[m][tm_ref[j]]
        c_ref[m, rows_of(col, slab), :] = t_refs[m][col]
        for p in targets:
            remote(
                t_refs[m].at[p], c_ref.at[m, rows_of(col, slab), :],
                p2_send.at[m], p2_recv.at[m], {"col": p},
            )

    def phase2_done(m):
        drain(t_refs[m].at[pl.ds(0, cols - 1)], p2_recv.at[m])

    def invert(k):
        for i in range(blocks):
            for j in range(i + 1):
                u = g_ref[0, k, j * BLOCK : (j + 1) * BLOCK, i * BLOCK : (i + 1) * BLOCK]
                lf_ref[i * BLOCK : (i + 1) * BLOCK, j * BLOCK : (j + 1) * BLOCK] = (
                    u.astype(jnp.float32).T
                )
        r = lax.broadcasted_iota(jnp.int32, (BLOCK, BLOCK), 0)
        c = lax.broadcasted_iota(jnp.int32, (BLOCK, BLOCK), 1)
        eye = r == c
        diag = [
            lf_ref[i * BLOCK : (i + 1) * BLOCK, i * BLOCK : (i + 1) * BLOCK]
            for i in range(blocks)
        ]
        xs = [jnp.where(eye, 1.0 / jnp.where(eye, d, 1.0), 0.0) for d in diag]
        shift = 0
        while (1 << shift) < BLOCK:
            rb, cb = r >> shift, c >> shift
            mask = ((rb >> 1) == (cb >> 1)) & (rb > cb)
            mids = [dot_f32(x, jnp.where(mask, d, 0.0)) for x, d in zip(xs, diag)]
            xs = [x - dot_f32(mid, x) for x, mid in zip(xs, mids)]
            shift += 1
        for i in range(blocks):
            inv_ref[i] = xs[i]

    def solve(work, s_ref):
        for i in range(blocks):
            rng = slice(i * BLOCK, (i + 1) * BLOCK)
            r = work(rng)
            if i:
                r = r - dot_f32(lf_ref[rng, : i * BLOCK], x_ref[: i * BLOCK, :])
            x = dot_f32(inv_ref[i], r)
            x_ref[rng, :] = x
            s_ref[rng, :] = x.astype(jnp.bfloat16)

    def scatter(root, k, s_ref):
        def one(d, _):
            p = lax.rem(row + d, rows)
            remote(
                s_ref.at[rows_of(p, piece), :], s_ref.at[rows_of(p, piece), :],
                sc_send.at[k], sc_recv.at[k], {"row": p},
            )
            return 0

        lax.fori_loop(1, rows, one, 0)

    def gather(root, k, s_ref):
        @pl.when(row != root)
        def _():
            drain(s_ref.at[pl.ds(0, piece), :], sc_recv.at[k])

        mine = s_ref.at[rows_of(row, piece), :]

        def one(d, _):
            p = lax.rem(row + d, rows)

            @pl.when(p != root)
            def _():
                remote(mine, mine, ga_send.at[k], ga_recv.at[k], {"row": p})

            return 0

        lax.fori_loop(1, rows, one, 0)

    def gathered(root, k, s_ref):
        @pl.when(row != root)
        def _():
            drain(s_ref.at[pl.ds(0, tile - piece), :], ga_recv.at[k])

    def update(k, s_ref):
        def one(step, _):
            m, at = step // blocks, step % blocks
            cut = pl.ds(pl.multiple_of(at * BLOCK, BLOCK), BLOCK)
            term = dot_t(g_ref[m, k, :, cut], s_ref[...])
            if k == 0:
                acc_ref[m, cut, :] = term
            else:
                acc_ref[m, cut, :] = acc_ref[m, cut, :] + term
            return 0

        lax.fori_loop(0, tiles * blocks, one, 0)

    send_up(1)
    send_down(1)
    remote(lt_ref, panel(0), pair_send, pair_recv, partner)
    g_ref[:, :, rows_of(col, slab), :] = lt_ref[...]
    phase1(0)
    for step in range(1, far):
        arrive(step)
    phase1(1)
    phase2(0)
    phase1(2)
    arrive(far)
    drain(g_ref.at[:, :, pl.ds(0, tile // 2), :], pair_recv)

    @pl.when(row == 0)
    def _():
        invert(0)

    @pl.when(row == 1)
    def _():
        invert(1)

    phase2(1)
    phase2_done(0)

    @pl.when(row == 0)
    def _():
        solve(lambda rng: c_ref[0, rng, :].astype(jnp.float32), s0_ref)
        scatter(0, 0, s0_ref)

    gather(0, 0, s0_ref)
    phase2(2)
    gathered(0, 0, s0_ref)
    update(0, s0_ref)

    @pl.when(row == 1)
    def _():
        solve(lambda rng: c_ref[0, rng, :].astype(jnp.float32) - acc_ref[0, rng, :], s1_ref)
        scatter(1, 1, s1_ref)

    gather(1, 1, s1_ref)
    gathered(1, 1, s1_ref)
    update(1, s1_ref)

    for m in range(tiles):
        if m:
            phase2_done(m)
        out_ref[m] = (c_ref[m].astype(jnp.float32) - acc_ref[m]).astype(jnp.bfloat16)

    @pl.when(row == 0)
    def _():
        out_ref[0] = s0_ref[...]

    @pl.when(row == 1)
    def _():
        out_ref[0] = s1_ref[...]

    for step in range(1, far + 1):
        drain(panel(0, 0 if step == far else None), up_send.at[step - 1])
        drain(panel(0, 1 if step == far else None), down_send.at[step - 1])
    drain(g_ref.at[:, :, pl.ds(0, tile // 2), :], pair_send)
    for m in range(tiles):
        drain(a_refs[m].at[pl.ds(0, cols - 1)], p1_send.at[m])
        drain(t_refs[m].at[pl.ds(0, cols - 1)], p2_send.at[m])
    for k, (root, s_ref) in enumerate(((0, s0_ref), (1, s1_ref))):
        @pl.when(row == root)
        def _():
            drain(s_ref.at[pl.ds(0, tile - piece), :], sc_send.at[k])
            drain(s_ref.at[pl.ds(0, tile - piece), :], ga_send.at[k])

        @pl.when(row != root)
        def _():
            drain(s_ref.at[pl.ds(0, tile - 2 * piece), :], ga_send.at[k])


def body(rows, cols, lower, rhs, tile_map):
    rhs = rhs[0]
    panels = jnp.transpose(lower[0], (0, 2, 3, 1))
    tiles, tile, width = rhs.shape
    slab = tile // cols
    far = cols // 4
    vmem = pl.BlockSpec(memory_space=pltpu.VMEM)
    dma = pltpu.SemaphoreType.DMA
    lanes = [pltpu.VMEM((cols, slab, width), jnp.bfloat16) for _ in range(6)]
    out = pl.pallas_call(
        functools.partial(kernel, rows, cols),
        name="solve_step",
        out_shape=jax.ShapeDtypeStruct(rhs.shape, jnp.bfloat16),
        in_specs=[pl.BlockSpec(memory_space=pltpu.SMEM), vmem, vmem],
        out_specs=vmem,
        scratch_shapes=[
            *lanes,
            pltpu.VMEM((tiles, tile, width), jnp.bfloat16),
            pltpu.VMEM((tiles, 2, tile, tile), jnp.bfloat16),
            pltpu.VMEM((tile, width), jnp.bfloat16),
            pltpu.VMEM((tile, width), jnp.bfloat16),
            pltpu.VMEM((tiles, tile, width), jnp.float32),
            pltpu.VMEM((tile, tile), jnp.float32),
            pltpu.VMEM((tile // BLOCK, BLOCK, BLOCK), jnp.float32),
            pltpu.VMEM((tile, width), jnp.float32),
            dma((tiles,)), dma((tiles,)), dma((tiles,)), dma((tiles,)),
            dma((far,)), dma((far,)), dma((far,)), dma((far,)),
            dma, dma,
            dma((2,)), dma((2,)), dma((2,)), dma((2,)),
        ],
        compiler_params=pltpu.CompilerParams(
            collective_id=0, has_side_effects=True, vmem_limit_bytes=60 * 1024 * 1024
        ),
    )(tile_map, rhs, panels)
    return out[None]


def solution(mesh):
    rows, cols = mesh.shape["row"], mesh.shape["col"]
    return jax.shard_map(
        functools.partial(body, rows, cols),
        mesh=mesh,
        in_specs=(P("row", None, None, None, "col"), P("row", None, None, "col"), P()),
        out_specs=P("row", None, None, "col"),
        check_vma=False,
    )
```

time: 524 us -> 140 us (0.27)
  the two profiles are of different devices: /device:TPU:1 before, /device:TPU:16 now
where the time goes in v1:
time: 140 us
  Pallas kernels  137 us (98%)
  local copies, waits for them, and re-layouts  2.65 us (2%)
    pallas_call x1, Pallas kernels, body(): pl.pallas_call(functools.partial(kernel, rows, cols), name='solve_step',...  137 us

profile of v1, /device:TPU:16, one launch (start us, length us, event | category | flops | bytes accessed | tf_op | source)
XLA Modules:
  0.0 139.5 jit_solution(18027658291511626243)
XLA Ops:
  0.0 136.9 %solve_step.1 = bf16[3,512,512]{2,1,0:T(8,128)(2,1)} custom-call(s32[16]{0:T(128)} %tm_ref.1, bf16[3,512,512]{2,1,0:T(8,128)(2,1)} %bitcast.6, bf16[3,2,32,512]{3,2,1,0:T(8,128)(2,1)} %bitcast.7), custom_call_target="tpu_custom_call" | custom-call | tf_op jit(solution)/shard_map/solve_step/pallas_call | solution.py:303
  136.9 2.7 %copy.5 = bf16[1,3,512,512]{3,2,1,0:T(8,128)(2,1)} copy(bf16[1,3,512,512]{3,2,1,0:T(8,128)(2,1)} %bitcast.5) | data formatting | bytes 3145728

commit v2 on v1

v2 whole, which is shorter than its diff:
```python
import functools

import jax
import jax.numpy as jnp
from jax import lax
from jax.experimental import pallas as pl
from jax.experimental.pallas import tpu as pltpu
from jax.sharding import PartitionSpec as P

MESH = pl.DeviceIdType.MESH
BLOCK = 128
VMEM_BYTES = 32 * 1024 * 1024
HIGHEST = lax.Precision.HIGHEST


def dot_f32(a, b):
    return jnp.dot(a, b, preferred_element_type=jnp.float32, precision=HIGHEST)


def halves(a):
    high = a.astype(jnp.bfloat16)
    return high, (a - high.astype(jnp.float32)).astype(jnp.bfloat16)


def dot(a, b):
    return jnp.dot(a, b, preferred_element_type=jnp.float32)


def farthest_first(size):
    return sorted(range(1, size), key=lambda d: -min(d, size - d))


def kernel(
    rows, cols, wide, tm_ref, rhs_ref, lt_ref, out_ref,
    a0, a1, a2, t0, t1, t2, c_ref, g_ref, l_ref, s0_ref, s1_ref, acc_ref, lf_ref, inv_ref, xh_ref, xl_ref,
    p1_send, p1_recv, p2_send, p2_recv, up_send, up_recv, down_send, down_recv,
    pair_send, pair_recv, sc_send, sc_recv, gz_send, gz_recv, gx_send, gx_recv,
):
    a_refs, t_refs = (a0, a1, a2), (t0, t1, t2)
    tiles, tile = rhs_ref.shape[0], rhs_ref.shape[1]
    slab, piece = tile // cols, tile // rows
    chips = cols // 2
    far = chips // 2
    blocks = tile // BLOCK
    row, col = lax.axis_index("row"), lax.axis_index("col")
    chip, core = col // 2, col % 2
    deep = rows // wide
    z, x = row // wide, row % wide

    barrier = pltpu.get_barrier_semaphore()

    def greet_col(d, _):
        pl.semaphore_signal(
            barrier, inc=1, device_id={"col": lax.rem(col + d, cols)}, device_id_type=MESH
        )
        return 0

    def greet_row(d, _):
        pl.semaphore_signal(
            barrier, inc=1, device_id={"row": lax.rem(row + d, rows)}, device_id_type=MESH
        )
        return 0

    lax.fori_loop(1, cols, greet_col, 0)
    lax.fori_loop(1, rows, greet_row, 0)
    g_ref[:, :, pl.ds(pl.multiple_of(col * slab, slab), slab), :] = lt_ref[...]
    pl.semaphore_wait(barrier, cols + rows - 2)

    def at_chip(offset):
        return lax.rem(chip + offset + 2 * chips, chips) * 2 + core

    def rows_of(index, size):
        return pl.ds(pl.multiple_of(index * size, size), size)

    def remote(src, dst, send, recv, target):
        copy = pltpu.make_async_remote_copy(
            src_ref=src, dst_ref=dst, send_sem=send, recv_sem=recv,
            device_id=target, device_id_type=MESH,
        )
        copy.start()

    def drain(ref, sem):
        pltpu.make_async_copy(ref, ref, sem).wait()

    partner = {"col": chip * 2 + 1 - core}

    def panel(ref, part, where, half=None):
        which = 0 if part == 0 else pl.ds(1, tiles - 1)
        if half is None:
            return ref.at[which, :, where, :]
        return ref.at[which, half, where, :]

    def ring_send(part, step, sign):
        half = (0 if sign > 0 else 1) if step == far else None
        block = panel(g_ref, part, rows_of(at_chip(sign * (1 - step)), slab), half)
        src = panel(lt_ref, part, slice(None), half) if step == 1 else block
        send, recv = (up_send, up_recv) if sign > 0 else (down_send, down_recv)
        remote(
            src, block, send.at[part, step - 1], recv.at[part, step - 1], {"col": at_chip(sign)}
        )

    def ring_start(part):
        ring_send(part, 1, 1)
        ring_send(part, 1, -1)
        remote(
            panel(lt_ref, part, slice(None)), panel(g_ref, part, rows_of(col, slab)),
            pair_send.at[part], pair_recv.at[part], partner,
        )

    def ring_block(part, step, sign):
        half = (0 if sign > 0 else 1) if step == far else None
        return panel(g_ref, part, rows_of(at_chip(-sign * step), slab), half)

    def ring_step(part, step):
        for sign, recv in ((1, up_recv), (-1, down_recv)):
            block = ring_block(part, step, sign)
            drain(block, recv.at[part, step - 1])
            if step < far:
                ring_send(part, step + 1, sign)
            remote(block, block, pair_send.at[part], pair_recv.at[part], partner)

    def ring_paired(part, sem):
        drain(panel(g_ref, part, pl.ds(0, tile // 2)), sem.at[part])

    order = []
    for d in range(far, 0, -1):
        order += [d] if d in (far,) else [d, chips - d]
    targets = []
    for d in order:
        targets.append(lax.rem(chip + d, chips) * 2 + core)
        targets.append(lax.rem(chip + d, chips) * 2 + 1 - core)
    targets.append(chip * 2 + 1 - core)

    def phase1(m, some):
        for p in some:
            remote(
                rhs_ref.at[m, rows_of(p, slab), :], a_refs[m].at[col],
                p1_send.at[m], p1_recv.at[m], {"col": p},
            )
        if some is targets or some[-1] is targets[-1]:
            a_refs[m][col] = rhs_ref[m, rows_of(col, slab), :]

    def phase2(m):
        drain(a_refs[m].at[pl.ds(0, cols - 1)], p1_recv.at[m])
        for j in range(cols):
            t_refs[m][j] = a_refs[m][tm_ref[j]]
        c_ref[m, rows_of(col, slab), :] = t_refs[m][col]
        for p in targets:
            remote(
                t_refs[m].at[p], c_ref.at[m, rows_of(col, slab), :],
                p2_send.at[m], p2_recv.at[m], {"col": p},
            )

    def phase2_done(m):
        drain(t_refs[m].at[pl.ds(0, cols - 1)], p2_recv.at[m])

    def invert(k):
        for i in range(blocks):
            for j in range(i + 1):
                u = g_ref[0, k, j * BLOCK : (j + 1) * BLOCK, i * BLOCK : (i + 1) * BLOCK]
                lf_ref[i * BLOCK : (i + 1) * BLOCK, j * BLOCK : (j + 1) * BLOCK] = (
                    u.astype(jnp.float32).T
                )
        r = lax.broadcasted_iota(jnp.int32, (BLOCK, BLOCK), 0)
        c = lax.broadcasted_iota(jnp.int32, (BLOCK, BLOCK), 1)
        eye = r == c
        diag = [
            lf_ref[i * BLOCK : (i + 1) * BLOCK, i * BLOCK : (i + 1) * BLOCK]
            for i in range(blocks)
        ]
        xs = [jnp.where(eye, 1.0 / jnp.where(eye, d, 1.0), 0.0) for d in diag]
        shift = 0
        while (1 << shift) < BLOCK:
            rb, cb = r >> shift, c >> shift
            mask = ((rb >> 1) == (cb >> 1)) & (rb > cb)
            mids = [dot_f32(x, jnp.where(mask, d, 0.0)) for x, d in zip(xs, diag)]
            xs = [x - dot_f32(mid, x) for x, mid in zip(xs, mids)]
            shift += 1
        for i in range(blocks):
            inv_ref[i] = xs[i]

    def solve(work, s_ref):
        for i in range(blocks):
            rng = slice(i * BLOCK, (i + 1) * BLOCK)
            r = work(rng)
            if i:
                left = lf_ref[rng, : i * BLOCK].astype(jnp.bfloat16)
                r = r - (dot(left, xh_ref[: i * BLOCK, :]) + dot(left, xl_ref[: i * BLOCK, :]))
            ih, il = halves(inv_ref[i])
            rh, rl = halves(r)
            sol = dot(ih, rh) + (dot(ih, rl) + dot(il, rh))
            xh_ref[rng, :], xl_ref[rng, :] = halves(sol)
            for g in range(rng.start // piece, rng.stop // piece):
                at = g * piece - rng.start
                s_ref[g // wide, g % wide] = sol[at : at + piece].astype(jnp.bfloat16)

    def put(piece_ref, send, recv, target):
        remote(piece_ref, piece_ref, send, recv, target)

    def scatter(k, s_ref):
        def hops(p):
            dz, dx = abs(p // wide - k // wide), abs(p % wide - k % wide)
            return min(dz, deep - dz) + min(dx, wide - dx)

        for p in sorted((p for p in range(rows) if p != k), key=lambda p: -hops(p)):
            put(s_ref.at[p // wide, p % wide], sc_send.at[k], sc_recv.at[k], {"row": p})

    def gather_z(root, k, s_ref):
        @pl.when(row != root)
        def _():
            drain(s_ref.at[z, x], sc_recv.at[k])

        for d in farthest_first(deep):
            p = lax.rem(z + d, deep) * wide + x

            @pl.when(p != root)
            def _():
                put(s_ref.at[z, x], gz_send.at[k], gz_recv.at[k], {"row": p})

    def gather_x(root, k, s_ref):
        @pl.when(row != root)
        def _():
            drain(s_ref.at[pl.ds(0, deep - 1), 0], gz_recv.at[k])

        for d in farthest_first(wide):
            p = z * wide + lax.rem(x + d, wide)

            @pl.when(p != root)
            def _():
                put(s_ref.at[:, x], gx_send.at[k], gx_recv.at[k], {"row": p})

    def gathered(root, k, s_ref):
        @pl.when(row != root)
        def _():
            drain(s_ref.at[:, pl.ds(0, wide - 1)], gx_recv.at[k])

    def whole(s_ref):
        return s_ref[...].reshape(tile, s_ref.shape[-1])

    def transpose(m):
        for k in range(2):
            for i in range(blocks):
                cut = slice(i * BLOCK, (i + 1) * BLOCK)
                l_ref[m, k, cut, :] = g_ref[m, k, :, cut].T

    def update(m, k, s_ref):
        for i in range(blocks):
            cut = slice(i * BLOCK, (i + 1) * BLOCK)
            term = jnp.dot(l_ref[m, k, cut, :], whole(s_ref), preferred_element_type=jnp.float32)
            if k == 0:
                acc_ref[m, cut, :] = term
            else:
                acc_ref[m, cut, :] = acc_ref[m, cut, :] + term

    scope = jax.named_scope
    quarter = (len(targets) + 3) // 4
    parts = [targets[i * quarter : (i + 1) * quarter] for i in range(4)]
    with scope("start"):
        ring_start(0)
        phase1(0, parts[0])
    for step in range(1, far):
        with scope(f"r0_{step}"):
            ring_step(0, step)
            if parts[step]:
                phase1(0, parts[step])
    for step in range(far, 4):
        if parts[step]:
            phase1(0, parts[step])
    with scope("rr_start"):
        ring_start(1)
    with scope("p2_0"):
        phase2(0)
    with scope("r0_end"):
        ring_step(0, far)
        ring_paired(0, pair_recv)

    @pl.when(row == 0)
    def _():
        with scope("inv0"):
            invert(0)

    @pl.when(row == 1)
    def _():
        with scope("inv1"):
            invert(1)

    with scope("rr1"):
        ring_step(1, 1)
        phase1(1, targets)
    with scope("p2_0_done"):
        phase2_done(0)

    @pl.when(row == 0)
    def _():
        with scope("solve0"):
            solve(lambda rng: c_ref[0, rng, :].astype(jnp.float32), s0_ref)
            scatter(0, s0_ref)

    with scope("tr0"):
        transpose(0)
    with scope("rr2"):
        if far > 2:
            ring_step(1, 2)
        phase1(2, targets)
    with scope("gz0"):
        gather_z(0, 0, s0_ref)
    with scope("gx0"):
        gather_x(0, 0, s0_ref)
    with scope("p2_1"):
        phase2(1)
    with scope("rr3"):
        if far > 3:
            ring_step(1, 3)
    with scope("gx0_done"):
        gathered(0, 0, s0_ref)
    with scope("up00"):
        update(0, 0, s0_ref)

    @pl.when(row == 1)
    def _():
        with scope("solve1"):
            solve(lambda rng: c_ref[0, rng, :].astype(jnp.float32) - acc_ref[0, rng, :], s1_ref)
            scatter(1, s1_ref)

    with scope("gz1"):
        gather_z(1, 1, s1_ref)
    with scope("p2_2"):
        phase2(2)
    with scope("gx1"):
        gather_x(1, 1, s1_ref)
    with scope("rr_end"):
        ring_step(1, far)
    with scope("rr_pair"):
        ring_paired(1, pair_recv)
    with scope("tr12"):
        for m in range(1, tiles):
            transpose(m)
    with scope("up0"):
        for m in range(1, tiles):
            update(m, 0, s0_ref)
    with scope("gx1_done"):
        gathered(1, 1, s1_ref)

    for m in range(tiles):
        with scope(f"up1{m}"):
            update(m, 1, s1_ref)
        with scope(f"fin{m}"):
            if m:
                phase2_done(m)
        with scope(f"out{m}"):
            out_ref[m] = (c_ref[m].astype(jnp.float32) - acc_ref[m]).astype(jnp.bfloat16)

    @pl.when(row == 0)
    def _():
        out_ref[0] = whole(s0_ref)

    @pl.when(row == 1)
    def _():
        out_ref[0] = whole(s1_ref)

    for part in range(2):
        for step in range(1, far + 1):
            drain(ring_block(part, step, 1), up_send.at[part, step - 1])
            drain(ring_block(part, step, -1), down_send.at[part, step - 1])
        ring_paired(part, pair_send)
    for m in range(tiles):
        drain(a_refs[m].at[pl.ds(0, cols - 1)], p1_send.at[m])
        drain(t_refs[m].at[pl.ds(0, cols - 1)], p2_send.at[m])

    def pieces(n):
        return c_ref.at[0, pl.ds(0, n * piece), :]

    for root in range(2):
        near_z = (x == root % wide) & (row != root)
        near_x = (z == root // wide) & (row != root)

        @pl.when(row == root)
        def _():
            drain(pieces(rows - 1), sc_send.at[root])

        for near, sem, count, each in (
            (near_z, gz_send, deep - 1, 1), (near_x, gx_send, wide - 1, deep),
        ):
            if count > 1:
                @pl.when(near)
                def _():
                    drain(pieces((count - 1) * each), sem.at[root])

            @pl.when(jnp.logical_not(near))
            def _():
                drain(pieces(count * each), sem.at[root])


def body(rows, cols, wide, lower, rhs, tile_map):
    rhs = rhs[0]
    panels = jnp.transpose(lower[0], (0, 2, 3, 1))
    tiles, tile, width = rhs.shape
    slab = tile // cols
    far = cols // 4
    vmem = pl.BlockSpec(memory_space=pltpu.VMEM)
    dma = pltpu.SemaphoreType.DMA
    lanes = [pltpu.VMEM((cols, slab, width), jnp.bfloat16) for _ in range(6)]
    out = pl.pallas_call(
        functools.partial(kernel, rows, cols, wide),
        name="solve_step",
        out_shape=jax.ShapeDtypeStruct(rhs.shape, jnp.bfloat16),
        in_specs=[pl.BlockSpec(memory_space=pltpu.SMEM), vmem, vmem],
        out_specs=vmem,
        scratch_shapes=[
            *lanes,
            pltpu.VMEM((tiles, tile, width), jnp.bfloat16),
            pltpu.VMEM((tiles, 2, tile, tile), jnp.bfloat16),
            pltpu.VMEM((tiles, 2, tile, tile), jnp.bfloat16),
            pltpu.VMEM((rows // wide, wide, tile // rows, width), jnp.bfloat16),
            pltpu.VMEM((rows // wide, wide, tile // rows, width), jnp.bfloat16),
            pltpu.VMEM((tiles, tile, width), jnp.float32),
            pltpu.VMEM((tile, tile), jnp.float32),
            pltpu.VMEM((tile // BLOCK, BLOCK, BLOCK), jnp.float32),
            pltpu.VMEM((tile, width), jnp.bfloat16),
            pltpu.VMEM((tile, width), jnp.bfloat16),
            dma((tiles,)), dma((tiles,)), dma((tiles,)), dma((tiles,)),
            dma((2, far)), dma((2, far)), dma((2, far)), dma((2, far)),
            dma((2,)), dma((2,)),
            dma((2,)), dma((2,)), dma((2,)), dma((2,)), dma((2,)), dma((2,)),
        ],
        compiler_params=pltpu.CompilerParams(
            collective_id=0, has_side_effects=True, vmem_limit_bytes=VMEM_BYTES
        ),
    )(tile_map, rhs, panels)
    return out[None]


def solution(mesh):
    rows, cols = mesh.shape["row"], mesh.shape["col"]
    wide = 4 if rows % 16 == 0 else 2
    return jax.shard_map(
        functools.partial(body, rows, cols, wide),
        mesh=mesh,
        in_specs=(P("row", None, None, None, "col"), P("row", None, None, "col"), P()),
        out_specs=P("row", None, None, "col"),
        check_vma=False,
    )
```

time: 140 us -> 109 us (0.78)
  the two profiles are of different devices: /device:TPU:16 before, /device:TPU:1 now
where the time goes in v2:
time: 109 us; the launch traced here: 108 us
  Pallas kernels  104 us (95%)
  local copies, waits for them, and re-layouts  4.13 us (4%)
    pallas_call x1, Pallas kernels, body(): pl.pallas_call(functools.partial(kernel, rows, cols, wide), name='solve_s...  104 us
    unnamed x7, local copies, waits for them, and re-layouts  4.13 us

profile of v2, /device:TPU:1, one launch (start us, length us, event | category | flops | bytes accessed | tf_op | source)
XLA Modules:
  0.0 108.4 jit_solution(16067424670971700148)
XLA Ops:
  0.0 0.0 copy-start
  0.0 1.4 %copy-done = bf16[1,3,512,512]{3,2,1,0:T(8,128)(2,1)S(1)} copy-done((bf16[1,3,512,512]{3,2,1,0:T(8,128)(2,1)S(1)}, bf16[1,3,512,512]{3,2,1,0:T(8,128)(2,1)}, u32[]{:S(2)}) %copy-start) | copy-done | bytes 1572888
  1.4 0.0 copy-start.1
  1.4 0.9 copy-done.1
  2.3 0.0 copy-start.2
  2.3 0.7 copy-done.2
  3.0 104.2 %solve_step.1 = bf16[3,512,512]{2,1,0:T(8,128)(2,1)S(1)} custom-call(s32[16]{0:T(128)S(1)} %copy-done.2, bf16[3,512,512]{2,1,0:T(8,128)(2,1)S(1)} %bitcast.6, bf16[3,2,32,512]{3,2,1,0:T(8,128)(2,1)S(1)} %bitcast.7), custom_call_target="tpu_custom_call" | custom-call | tf_op jit(solution)/shard_map/solve_step/pallas_call | solution.py:403
  107.2 1.1 %copy.5 = bf16[1,3,512,512]{3,2,1,0:T(8,128)(2,1)} copy(bf16[1,3,512,512]{3,2,1,0:T(8,128)(2,1)S(1)} %bitcast.5) | data formatting | bytes 3145728
Async XLA Ops:
  0.0 1.4 %copy-start = (bf16[1,3,512,512]{3,2,1,0:T(8,128)(2,1)S(1)}, bf16[1,3,512,512]{3,2,1,0:T(8,128)(2,1)}, u32[]{:S(2)}) copy-start(bf16[1,3,512,512]{3,2,1,0:T(8,128)(2,1)} %param.4) | copy-start | bytes 4718596
  1.4 0.9 copy-start.1
  2.3 0.7 copy-start.2

commit v3 on v2

--- a/solution.py
+++ b/solution.py
@@ -9,7 +9,7 @@
 
 MESH = pl.DeviceIdType.MESH
 BLOCK = 128
-VMEM_BYTES = 32 * 1024 * 1024
+VMEM_BYTES = 54_000_000
 HIGHEST = lax.Precision.HIGHEST
 
 
@@ -31,10 +31,10 @@
 
 
 def kernel(
-    rows, cols, wide, tm_ref, rhs_ref, lt_ref, out_ref,
+    rows, cols, wide, tm_hbm, rhs_hbm, lt_hbm, out_ref, tm_ref, rhs_ref, lt_ref,
     a0, a1, a2, t0, t1, t2, c_ref, g_ref, l_ref, s0_ref, s1_ref, acc_ref, lf_ref, inv_ref, xh_ref, xl_ref,
     p1_send, p1_recv, p2_send, p2_recv, up_send, up_recv, down_send, down_recv,
-    pair_send, pair_recv, sc_send, sc_recv, gz_send, gz_recv, gx_send, gx_recv,
+    pair_send, pair_recv, sc_send, sc_recv, gz_send, gz_recv, gx_send, gx_recv, in_sem, ready,
 ):
     a_refs, t_refs = (a0, a1, a2), (t0, t1, t2)
     tiles, tile = rhs_ref.shape[0], rhs_ref.shape[1]
@@ -47,24 +47,30 @@
     deep = rows // wide
     z, x = row // wide, row % wide
 
+    load_lt = pltpu.make_async_copy(lt_hbm, lt_ref, in_sem.at[0])
+    load_rhs = pltpu.make_async_copy(rhs_hbm, rhs_ref, in_sem.at[1])
+    load_tm = pltpu.make_async_copy(tm_hbm, tm_ref, in_sem.at[2])
+    for load in (load_lt, load_rhs, load_tm):
+        load.start()
+
     barrier = pltpu.get_barrier_semaphore()
 
-    def greet_col(d, _):
-        pl.semaphore_signal(
-            barrier, inc=1, device_id={"col": lax.rem(col + d, cols)}, device_id_type=MESH
-        )
-        return 0
-
-    def greet_row(d, _):
-        pl.semaphore_signal(
-            barrier, inc=1, device_id={"row": lax.rem(row + d, rows)}, device_id_type=MESH
-        )
-        return 0
-
-    lax.fori_loop(1, cols, greet_col, 0)
-    lax.fori_loop(1, rows, greet_row, 0)
-    g_ref[:, :, pl.ds(pl.multiple_of(col * slab, slab), slab), :] = lt_ref[...]
-    pl.semaphore_wait(barrier, cols + rows - 2)
+    def greet(target):
+        pl.semaphore_signal(barrier, inc=1, device_id=target, device_id_type=MESH)
+
+    for d in farthest_first(cols):
+        greet({"col": lax.rem(col + d, cols)})
+    for d in farthest_first(deep):
+        greet({"row": lax.rem(z + d, deep) * wide + x})
+    for d in farthest_first(wide):
+        greet({"row": z * wide + lax.rem(x + d, wide)})
+    pl.semaphore_wait(barrier, cols + deep + wide - 3)
+    for root in range(2):
+        @pl.when((x == root) & (z != 0))
+        def _():
+            pl.semaphore_signal(
+                ready.at[root], inc=1, device_id={"row": root}, device_id_type=MESH
+            )
 
     def at_chip(offset):
         return lax.rem(chip + offset + 2 * chips, chips) * 2 + core
@@ -198,6 +204,8 @@
         remote(piece_ref, piece_ref, send, recv, target)
 
     def scatter(k, s_ref):
+        pl.semaphore_wait(ready.at[k], deep - 1)
+
         def hops(p):
             dz, dx = abs(p // wide - k // wide), abs(p % wide - k % wide)
             return min(dz, deep - dz) + min(dx, wide - dx)
@@ -256,20 +264,30 @@
     quarter = (len(targets) + 3) // 4
     parts = [targets[i * quarter : (i + 1) * quarter] for i in range(4)]
     with scope("start"):
+        load_lt.wait()
         ring_start(0)
+        load_rhs.wait()
         phase1(0, parts[0])
-    for step in range(1, far):
-        with scope(f"r0_{step}"):
-            ring_step(0, step)
-            if parts[step]:
-                phase1(0, parts[step])
-    for step in range(far, 4):
-        if parts[step]:
-            phase1(0, parts[step])
+        phase1(0, parts[1])
+        g_ref[:, :, rows_of(col, slab), :] = lt_ref[...]
+    with scope("r0_1"):
+        ring_step(0, 1)
+        phase1(0, parts[2])
+        phase1(0, parts[3])
+    if far > 2:
+        with scope("r0_2"):
+            ring_step(0, 2)
     with scope("rr_start"):
         ring_start(1)
+    if far > 3:
+        with scope("r0_3"):
+            ring_step(0, 3)
+    load_tm.wait()
     with scope("p2_0"):
         phase2(0)
+    with scope("rr1"):
+        ring_step(1, 1)
+        phase1(1, targets)
     with scope("r0_end"):
         ring_step(0, far)
         ring_paired(0, pair_recv)
@@ -284,9 +302,6 @@
         with scope("inv1"):
             invert(1)
 
-    with scope("rr1"):
-        ring_step(1, 1)
-        phase1(1, targets)
     with scope("p2_0_done"):
         phase2_done(0)
 
@@ -404,9 +419,12 @@
         functools.partial(kernel, rows, cols, wide),
         name="solve_step",
         out_shape=jax.ShapeDtypeStruct(rhs.shape, jnp.bfloat16),
-        in_specs=[pl.BlockSpec(memory_space=pltpu.SMEM), vmem, vmem],
+        in_specs=[pl.BlockSpec(memory_space=pl.ANY)] * 3,
         out_specs=vmem,
         scratch_shapes=[
+            pltpu.SMEM(tile_map.shape, jnp.int32),
+            pltpu.VMEM(rhs.shape, jnp.bfloat16),
+            pltpu.VMEM(panels.shape, jnp.bfloat16),
             *lanes,
             pltpu.VMEM((tiles, tile, width), jnp.bfloat16),
             pltpu.VMEM((tiles, 2, tile, tile), jnp.bfloat16),
@@ -422,6 +440,7 @@
             dma((2, far)), dma((2, far)), dma((2, far)), dma((2, far)),
             dma((2,)), dma((2,)),
             dma((2,)), dma((2,)), dma((2,)), dma((2,)), dma((2,)), dma((2,)),
+            dma((3,)), pltpu.SemaphoreType.REGULAR((2,)),
         ],
         compiler_params=pltpu.CompilerParams(
             collective_id=0, has_side_effects=True, vmem_limit_bytes=VMEM_BYTES

time: 109 us -> 101 us (0.927)
  Pallas kernels: 104 us -> 98.3 us
  local copies, waits for them, and re-layouts: 4.13 us -> 2.73 us
    pallas_call x1, Pallas kernels: 104 us -> 98.3 us  [body(): pl.pallas_call(functools.partial(kernel, rows, cols, wide), name='solve_s...]
    unnamed x7 -> x5, local copies, waits for them, and re-layouts: 4.13 us -> 2.73 us
where the time goes in v3:
time: 101 us
  Pallas kernels  98.3 us (97%)
  local copies, waits for them, and re-layouts  2.73 us (3%)
    pallas_call x1, Pallas kernels, body(): pl.pallas_call(functools.partial(kernel, rows, cols, wide), name='solve_s...  98.3 us
    unnamed x5, local copies, waits for them, and re-layouts  2.73 us

profile of v3, /device:TPU:1, one launch (start us, length us, event | category | flops | bytes accessed | tf_op | source)
XLA Modules:
  0.0 101.0 jit_solution(5227430003663737913)
XLA Ops:
  0.0 0.0 copy-start
  0.0 0.9 copy-done
  0.9 0.0 copy-start.1
  0.9 0.7 copy-done.1
  1.6 98.3 %solve_step.1 = bf16[3,512,512]{2,1,0:T(8,128)(2,1)S(1)} custom-call(s32[16]{0:T(128)S(1)} %copy-done.1, bf16[3,512,512]{2,1,0:T(8,128)(2,1)} %bitcast.7, bf16[3,2,32,512]{3,2,1,0:T(8,128)(2,1)S(1)} %bitcast.6), custom_call_target="tpu_custom_call" | custom-call | tf_op jit(solution)/shard_map/solve_step/pallas_call | solution.py:418
  99.9 1.1 %copy.5 = bf16[1,3,512,512]{3,2,1,0:T(8,128)(2,1)} copy(bf16[1,3,512,512]{3,2,1,0:T(8,128)(2,1)S(1)} %bitcast.5) | data formatting | bytes 3145728
Async XLA Ops:
  0.0 0.9 copy-start
  0.9 0.7 copy-start.1

commit v4 on v3

--- a/solution.py
+++ b/solution.py
@@ -9,7 +9,7 @@
 
 MESH = pl.DeviceIdType.MESH
 BLOCK = 128
-VMEM_BYTES = 54_000_000
+VMEM_BYTES = 58_000_000
 HIGHEST = lax.Precision.HIGHEST
 
 
@@ -34,7 +34,7 @@
     rows, cols, wide, tm_hbm, rhs_hbm, lt_hbm, out_ref, tm_ref, rhs_ref, lt_ref,
     a0, a1, a2, t0, t1, t2, c_ref, g_ref, l_ref, s0_ref, s1_ref, acc_ref, lf_ref, inv_ref, xh_ref, xl_ref,
     p1_send, p1_recv, p2_send, p2_recv, up_send, up_recv, down_send, down_recv,
-    pair_send, pair_recv, sc_send, sc_recv, gz_send, gz_recv, gx_send, gx_recv, in_sem, ready,
+    pair_send, pair_recv, sc_send, sc_recv, gz_send, gz_recv, gx_send, gx_recv, in_sem, ready, seen,
 ):
     a_refs, t_refs = (a0, a1, a2), (t0, t1, t2)
     tiles, tile = rhs_ref.shape[0], rhs_ref.shape[1]
@@ -55,22 +55,41 @@
 
     barrier = pltpu.get_barrier_semaphore()
 
-    def greet(target):
-        pl.semaphore_signal(barrier, inc=1, device_id=target, device_id_type=MESH)
+    def signal(sem, **target):
+        pl.semaphore_signal(sem, inc=1, device_id=target, device_id_type=MESH)
+
+    def along(sem, sign):
+        for d in range(1, deep):
+            at = z + sign * d
+
+            @pl.when((at >= 0) & (at < deep))
+            def _():
+                signal(sem, row=at * wide + x)
+
+        for d in range(1, wide):
+            side = x + sign * d
+
+            @pl.when((side >= 0) & (side < wide))
+            def _():
+                signal(sem, row=z * wide + side)
 
     for d in farthest_first(cols):
-        greet({"col": lax.rem(col + d, cols)})
-    for d in farthest_first(deep):
-        greet({"row": lax.rem(z + d, deep) * wide + x})
-    for d in farthest_first(wide):
-        greet({"row": z * wide + lax.rem(x + d, wide)})
-    pl.semaphore_wait(barrier, cols + deep + wide - 3)
-    for root in range(2):
-        @pl.when((x == root) & (z != 0))
+        signal(barrier, col=lax.rem(col + d, cols))
+    along(barrier, 1)
+    pl.semaphore_wait(barrier, cols - 1 + z + x)
+    along(seen, -1)
+
+    def meet():
+        higher = deep + wide - 2 - z - x
+
+        @pl.when(higher > 0)
         def _():
-            pl.semaphore_signal(
-                ready.at[root], inc=1, device_id={"row": root}, device_id_type=MESH
-            )
+            pl.semaphore_wait(seen, higher)
+
+        for root in range(2):
+            @pl.when((x == root) & (z != 0))
+            def _():
+                signal(ready.at[root], row=root)
 
     def at_chip(offset):
         return lax.rem(chip + offset + 2 * chips, chips) * 2 + core
@@ -279,6 +298,8 @@
             ring_step(0, 2)
     with scope("rr_start"):
         ring_start(1)
+    with scope("meet"):
+        meet()
     if far > 3:
         with scope("r0_3"):
             ring_step(0, 3)
@@ -418,7 +439,7 @@
     out = pl.pallas_call(
         functools.partial(kernel, rows, cols, wide),
         name="solve_step",
-        out_shape=jax.ShapeDtypeStruct(rhs.shape, jnp.bfloat16),
+        out_shape=pltpu.VMEM(rhs.shape, jnp.bfloat16),
         in_specs=[pl.BlockSpec(memory_space=pl.ANY)] * 3,
         out_specs=vmem,
         scratch_shapes=[
@@ -441,6 +462,7 @@
             dma((2,)), dma((2,)),
             dma((2,)), dma((2,)), dma((2,)), dma((2,)), dma((2,)), dma((2,)),
             dma((3,)), pltpu.SemaphoreType.REGULAR((2,)),
+            pltpu.SemaphoreType.REGULAR,
         ],
         compiler_params=pltpu.CompilerParams(
             collective_id=0, has_side_effects=True, vmem_limit_bytes=VMEM_BYTES

time: 101 us -> 95.7 us (0.948)
  Pallas kernels: 98.3 us -> 94.5 us
  local copies, waits for them, and re-layouts: 2.73 us -> 1.15 us
    pallas_call x1, Pallas kernels: 98.3 us -> 94.5 us  [body(): pl.pallas_call(functools.partial(kernel, rows, cols, wide), name='solve_s...]
    unnamed x5 -> x1, local copies, waits for them, and re-layouts: 2.73 us -> 1.15 us
where the time goes in v4:
time: 95.7 us; the launch traced here: 95.6 us
  Pallas kernels  94.5 us (99%)
  local copies, waits for them, and re-layouts  1.15 us (1%)
    pallas_call x1, Pallas kernels, body(): pl.pallas_call(functools.partial(kernel, rows, cols, wide), name='solve_s...  94.5 us

profile of v4, /device:TPU:1, one launch (start us, length us, event | category | flops | bytes accessed | tf_op | source)
XLA Modules:
  0.0 95.6 jit_solution(15514920521532853776)
XLA Ops:
  0.0 94.5 %solve_step.1 = bf16[3,512,512]{2,1,0:T(8,128)(2,1)S(1)} custom-call(s32[16]{0:T(128)} %tm_hbm.1, bf16[3,512,512]{2,1,0:T(8,128)(2,1)} %bitcast.6, bf16[3,2,32,512]{3,2,1,0:T(8,128)(2,1)} %bitcast.7), custom_call_target="tpu_custom_call" | custom-call | tf_op jit(solution)/shard_map/solve_step/pallas_call | solution.py:439
  94.5 1.1 %copy.5 = bf16[1,3,512,512]{3,2,1,0:T(8,128)(2,1)} copy(bf16[1,3,512,512]{3,2,1,0:T(8,128)(2,1)S(1)} %bitcast.5) | data formatting | bytes 3145728

commit v5 on v4

--- a/solution.py
+++ b/solution.py
@@ -34,7 +34,7 @@
     rows, cols, wide, tm_hbm, rhs_hbm, lt_hbm, out_ref, tm_ref, rhs_ref, lt_ref,
     a0, a1, a2, t0, t1, t2, c_ref, g_ref, l_ref, s0_ref, s1_ref, acc_ref, lf_ref, inv_ref, xh_ref, xl_ref,
     p1_send, p1_recv, p2_send, p2_recv, up_send, up_recv, down_send, down_recv,
-    pair_send, pair_recv, sc_send, sc_recv, gz_send, gz_recv, gx_send, gx_recv, in_sem, ready, seen,
+    pair_send, pair_recv, sc_send, sc_recv, gz_send, gz_recv, gx_send, gx_recv, in_sem, ready, seen, late,
 ):
     a_refs, t_refs = (a0, a1, a2), (t0, t1, t2)
     tiles, tile = rhs_ref.shape[0], rhs_ref.shape[1]
@@ -48,10 +48,13 @@
     z, x = row // wide, row % wide
 
     load_lt = pltpu.make_async_copy(lt_hbm, lt_ref, in_sem.at[0])
-    load_rhs = pltpu.make_async_copy(rhs_hbm, rhs_ref, in_sem.at[1])
+    load_rhs = pltpu.make_async_copy(rhs_hbm.at[0], rhs_ref.at[0], in_sem.at[1])
+    load_rest = pltpu.make_async_copy(
+        rhs_hbm.at[pl.ds(1, tiles - 1)], rhs_ref.at[pl.ds(1, tiles - 1)], in_sem.at[3]
+    )
     load_tm = pltpu.make_async_copy(tm_hbm, tm_ref, in_sem.at[2])
-    for load in (load_lt, load_rhs, load_tm):
-        load.start()
+    load_lt.start()
+    load_rhs.start()
 
     barrier = pltpu.get_barrier_semaphore()
 
@@ -73,11 +76,23 @@
             def _():
                 signal(sem, row=z * wide + side)
 
-    for d in farthest_first(cols):
-        signal(barrier, col=lax.rem(col + d, cols))
+    tardy = row == 0
+
+    @pl.when(jnp.logical_not(tardy & (col == 0)))
+    def _():
+        for d in farthest_first(cols):
+            signal(barrier, col=lax.rem(col + d, cols))
+
     along(barrier, 1)
-    pl.semaphore_wait(barrier, cols - 1 + z + x)
-    along(seen, -1)
+    load_rest.start()
+    load_tm.start()
+    pl.semaphore_wait(barrier, jnp.where(tardy & (col != 0), cols - 2, cols - 1) + z + x)
+
+    @pl.when(tardy & (col == 0))
+    def _():
+        for d in farthest_first(cols):
+            signal(late, col=d)
+
 
     def meet():
         higher = deep + wide - 2 - z - x
@@ -124,12 +139,23 @@
             src, block, send.at[part, step - 1], recv.at[part, step - 1], {"col": at_chip(sign)}
         )
 
-    def ring_start(part):
-        ring_send(part, 1, 1)
-        ring_send(part, 1, -1)
-        remote(
-            panel(lt_ref, part, slice(None)), panel(g_ref, part, rows_of(col, slab)),
-            pair_send.at[part], pair_recv.at[part], partner,
+    def ring_start(part, waited=None):
+        def send(target, act):
+            if waited is None:
+                act()
+            elif waited:
+                pl.when(tardy & (target == 0))(act)
+            else:
+                pl.when(jnp.logical_not(tardy & (target == 0)))(act)
+
+        send(at_chip(1), lambda: ring_send(part, 1, 1))
+        send(at_chip(-1), lambda: ring_send(part, 1, -1))
+        send(
+            chip * 2 + 1 - core,
+            lambda: remote(
+                panel(lt_ref, part, slice(None)), panel(g_ref, part, rows_of(col, slab)),
+                pair_send.at[part], pair_recv.at[part], partner,
+            ),
         )
 
     def ring_block(part, step, sign):
@@ -156,13 +182,19 @@
         targets.append(lax.rem(chip + d, chips) * 2 + 1 - core)
     targets.append(chip * 2 + 1 - core)
 
+    def hop1(m, p):
+        remote(
+            rhs_ref.at[m, rows_of(p, slab), :], a_refs[m].at[col],
+            p1_send.at[m], p1_recv.at[m], {"col": p},
+        )
+
     def phase1(m, some):
         for p in some:
-            remote(
-                rhs_ref.at[m, rows_of(p, slab), :], a_refs[m].at[col],
-                p1_send.at[m], p1_recv.at[m], {"col": p},
-            )
-        if some is targets or some[-1] is targets[-1]:
+            if m:
+                hop1(m, p)
+            else:
+                pl.when(jnp.logical_not(tardy & (p == 0)))(functools.partial(hop1, m, p))
+        if some[-1] is targets[-1]:
             a_refs[m][col] = rhs_ref[m, rows_of(col, slab), :]
 
     def phase2(m):
@@ -284,10 +316,18 @@
     parts = [targets[i * quarter : (i + 1) * quarter] for i in range(4)]
     with scope("start"):
         load_lt.wait()
-        ring_start(0)
+        ring_start(0, False)
         load_rhs.wait()
         phase1(0, parts[0])
+
+        @pl.when(tardy & (col != 0))
+        def _():
+            pl.semaphore_wait(late, 1)
+            hop1(0, 0)
+
+        ring_start(0, True)
         phase1(0, parts[1])
+        along(seen, -1)
         g_ref[:, :, rows_of(col, slab), :] = lt_ref[...]
     with scope("r0_1"):
         ring_step(0, 1)
@@ -306,6 +346,7 @@
     load_tm.wait()
     with scope("p2_0"):
         phase2(0)
+    load_rest.wait()
     with scope("rr1"):
         ring_step(1, 1)
         phase1(1, targets)
@@ -461,8 +502,8 @@
             dma((2, far)), dma((2, far)), dma((2, far)), dma((2, far)),
             dma((2,)), dma((2,)),
             dma((2,)), dma((2,)), dma((2,)), dma((2,)), dma((2,)), dma((2,)),
-            dma((3,)), pltpu.SemaphoreType.REGULAR((2,)),
-            pltpu.SemaphoreType.REGULAR,
+            dma((4,)), pltpu.SemaphoreType.REGULAR((2,)),
+            pltpu.SemaphoreType.REGULAR, pltpu.SemaphoreType.REGULAR,
         ],
         compiler_params=pltpu.CompilerParams(
             collective_id=0, has_side_effects=True, vmem_limit_bytes=VMEM_BYTES

time: 95.7 us -> 94.1 us (0.983)
  Pallas kernels: 94.5 us -> 92.9 us
    pallas_call x1, Pallas kernels: 94.5 us -> 92.9 us  [body(): pl.pallas_call(functools.partial(kernel, rows, cols, wide), name='solve_s...]
where the time goes in v5:
time: 94.1 us; the launch traced here: 94 us
  Pallas kernels  92.9 us (99%)
  local copies, waits for them, and re-layouts  1.15 us (1%)
    pallas_call x1, Pallas kernels, body(): pl.pallas_call(functools.partial(kernel, rows, cols, wide), name='solve_s...  92.9 us

profile of v5, /device:TPU:1, one launch (start us, length us, event | category | flops | bytes accessed | tf_op | source)
XLA Modules:
  0.0 94.0 jit_solution(12961602921884756079)
XLA Ops:
  0.0 92.9 %solve_step.1 = bf16[3,512,512]{2,1,0:T(8,128)(2,1)S(1)} custom-call(s32[16]{0:T(128)} %tm_hbm.1, bf16[3,512,512]{2,1,0:T(8,128)(2,1)} %bitcast.6, bf16[3,2,32,512]{3,2,1,0:T(8,128)(2,1)} %bitcast.7), custom_call_target="tpu_custom_call" | custom-call | tf_op jit(solution)/shard_map/solve_step/pallas_call | solution.py:480
  92.9 1.1 %copy.5 = bf16[1,3,512,512]{3,2,1,0:T(8,128)(2,1)} copy(bf16[1,3,512,512]{3,2,1,0:T(8,128)(2,1)S(1)} %bitcast.5) | data formatting | bytes 3145728

commit v6 on v5

--- a/solution.py
+++ b/solution.py
@@ -17,22 +17,13 @@
     return jnp.dot(a, b, preferred_element_type=jnp.float32, precision=HIGHEST)
 
 
-def halves(a):
-    high = a.astype(jnp.bfloat16)
-    return high, (a - high.astype(jnp.float32)).astype(jnp.bfloat16)
-
-
-def dot(a, b):
-    return jnp.dot(a, b, preferred_element_type=jnp.float32)
-
-
 def farthest_first(size):
     return sorted(range(1, size), key=lambda d: -min(d, size - d))
 
 
 def kernel(
     rows, cols, wide, tm_hbm, rhs_hbm, lt_hbm, out_ref, tm_ref, rhs_ref, lt_ref,
-    a0, a1, a2, t0, t1, t2, c_ref, g_ref, l_ref, s0_ref, s1_ref, acc_ref, lf_ref, inv_ref, xh_ref, xl_ref,
+    a0, a1, a2, t0, t1, t2, c_ref, g_ref, l_ref, s0_ref, s1_ref, acc_ref, lf_ref, inv_ref, x_ref,
     p1_send, p1_recv, p2_send, p2_recv, up_send, up_recv, down_send, down_recv,
     pair_send, pair_recv, sc_send, sc_recv, gz_send, gz_recv, gx_send, gx_recv, in_sem, ready, seen, late,
 ):
@@ -241,12 +232,9 @@
             rng = slice(i * BLOCK, (i + 1) * BLOCK)
             r = work(rng)
             if i:
-                left = lf_ref[rng, : i * BLOCK].astype(jnp.bfloat16)
-                r = r - (dot(left, xh_ref[: i * BLOCK, :]) + dot(left, xl_ref[: i * BLOCK, :]))
-            ih, il = halves(inv_ref[i])
-            rh, rl = halves(r)
-            sol = dot(ih, rh) + (dot(ih, rl) + dot(il, rh))
-            xh_ref[rng, :], xl_ref[rng, :] = halves(sol)
+                r = r - dot_f32(lf_ref[rng, : i * BLOCK], x_ref[: i * BLOCK, :])
+            sol = dot_f32(inv_ref[i], r)
+            x_ref[rng, :] = sol
             for g in range(rng.start // piece, rng.stop // piece):
                 at = g * piece - rng.start
                 s_ref[g // wide, g % wide] = sol[at : at + piece].astype(jnp.bfloat16)
@@ -496,8 +484,7 @@
             pltpu.VMEM((tiles, tile, width), jnp.float32),
             pltpu.VMEM((tile, tile), jnp.float32),
             pltpu.VMEM((tile // BLOCK, BLOCK, BLOCK), jnp.float32),
-            pltpu.VMEM((tile, width), jnp.bfloat16),
-            pltpu.VMEM((tile, width), jnp.bfloat16),
+            pltpu.VMEM((tile, width), jnp.float32),
             dma((tiles,)), dma((tiles,)), dma((tiles,)), dma((tiles,)),
             dma((2, far)), dma((2, far)), dma((2, far)), dma((2, far)),
             dma((2,)), dma((2,)),

time: 94.1 us -> 94.1 us (level)
  no operation moved by 1% of the time
where the time goes in v6:
time: 94.1 us; the launch traced here: 94 us
  Pallas kernels  92.9 us (99%)
  local copies, waits for them, and re-layouts  1.15 us (1%)
    pallas_call x1, Pallas kernels, body(): pl.pallas_call(functools.partial(kernel, rows, cols, wide), name='solve_s...  92.9 us

profile of v6, /device:TPU:1, one launch (start us, length us, event | category | flops | bytes accessed | tf_op | source)
XLA Modules:
  0.0 94.0 jit_solution(6291904732321616515)
XLA Ops:
  0.0 92.9 %solve_step.1 = bf16[3,512,512]{2,1,0:T(8,128)(2,1)S(1)} custom-call(s32[16]{0:T(128)} %tm_hbm.1, bf16[3,512,512]{2,1,0:T(8,128)(2,1)} %bitcast.6, bf16[3,2,32,512]{3,2,1,0:T(8,128)(2,1)} %bitcast.7), custom_call_target="tpu_custom_call" | custom-call | tf_op jit(solution)/shard_map/solve_step/pallas_call | solution.py:468
  92.9 1.1 %copy.5 = bf16[1,3,512,512]{3,2,1,0:T(8,128)(2,1)} copy(bf16[1,3,512,512]{3,2,1,0:T(8,128)(2,1)S(1)} %bitcast.5) | data formatting | bytes 3145728

commit v7 on v6

--- a/solution.py
+++ b/solution.py
@@ -409,11 +409,16 @@
     for m in range(tiles):
         with scope(f"up1{m}"):
             update(m, 1, s1_ref)
+
+    def finish(m):
+        out_ref[m] = (c_ref[m].astype(jnp.float32) - acc_ref[m]).astype(jnp.bfloat16)
+
+    for m in range(tiles - 1):
         with scope(f"fin{m}"):
             if m:
                 phase2_done(m)
         with scope(f"out{m}"):
-            out_ref[m] = (c_ref[m].astype(jnp.float32) - acc_ref[m]).astype(jnp.bfloat16)
+            finish(m)
 
     @pl.when(row == 0)
     def _():
@@ -430,7 +435,8 @@
         ring_paired(part, pair_send)
     for m in range(tiles):
         drain(a_refs[m].at[pl.ds(0, cols - 1)], p1_send.at[m])
-        drain(t_refs[m].at[pl.ds(0, cols - 1)], p2_send.at[m])
+        if m < tiles - 1:
+            drain(t_refs[m].at[pl.ds(0, cols - 1)], p2_send.at[m])
 
     def pieces(n):
         return c_ref.at[0, pl.ds(0, n * piece), :]
@@ -454,6 +460,13 @@
             @pl.when(jnp.logical_not(near))
             def _():
                 drain(pieces(count * each), sem.at[root])
+
+    last = tiles - 1
+    with scope("fin2"):
+        phase2_done(last)
+    with scope("out2"):
+        finish(last)
+    drain(t_refs[last].at[pl.ds(0, cols - 1)], p2_send.at[last])
 
 
 def body(rows, cols, wide, lower, rhs, tile_map):

time: 94.1 us -> 94.1 us (level)
  no operation moved by 1% of the time
where the time goes in v7:
time: 94.1 us; the launch traced here: 93.9 us
  Pallas kernels  92.8 us (99%)
  local copies, waits for them, and re-layouts  1.15 us (1%)
    pallas_call x1, Pallas kernels, body(): pl.pallas_call(functools.partial(kernel, rows, cols, wide), name='solve_s...  92.8 us

profile of v7, /device:TPU:1, one launch (start us, length us, event | category | flops | bytes accessed | tf_op | source)
XLA Modules:
  0.0 93.9 jit_solution(17480676401780688672)
XLA Ops:
  0.0 92.8 %solve_step.1 = bf16[3,512,512]{2,1,0:T(8,128)(2,1)S(1)} custom-call(s32[16]{0:T(128)} %tm_hbm.1, bf16[3,512,512]{2,1,0:T(8,128)(2,1)} %bitcast.6, bf16[3,2,32,512]{3,2,1,0:T(8,128)(2,1)} %bitcast.7), custom_call_target="tpu_custom_call" | custom-call | tf_op jit(solution)/shard_map/solve_step/pallas_call | solution.py:481
  92.8 1.1 %copy.5 = bf16[1,3,512,512]{3,2,1,0:T(8,128)(2,1)} copy(bf16[1,3,512,512]{3,2,1,0:T(8,128)(2,1)S(1)} %bitcast.5) | data formatting | bytes 3145728
